TPU v7x, 64 devices: a 2x2x8 block of a 4x4x8 slice. The times are simulated.
64 devices in a mesh: dp: 8 (over x, y, core), tp: 8 (over z).
Axes of the slice: x: 2, y: 2, z: 8, core: 2. Of those that a mesh axis runs over, the one named last changes fastest.
The devices are a block of a 4x4x8 slice.
Arguments:
- x: bfloat16 [16384, 3840], P('dp'), parts along dimension 0
- w_gate: bfloat16 [3840, 15360], P(None, 'tp')
- w_up: bfloat16 [3840, 15360], P(None, 'tp')
- w_down: bfloat16 [15360, 3840], P('tp')
Outputs:
- output: bfloat16 [16384, 3840], P('dp'), parts along dimension 0
There are 8 independent parts. A program takes and returns all parts, laid end to end along the dimension named above; an argument that names none is the same for every part.
All inputs are finite; a program needn't handle non-finite values.
Results may differ from a plain program's by a relative error of at most 0.016.
Values are sent between devices in bfloat16 or wider.
A program may use at most 768 MiB of HBM per device.

v0:
```python
import jax
import jax.numpy as jnp
from jax import lax
from jax.sharding import PartitionSpec as P


def solution(mesh):
    def step(x, w_gate, w_up, w_down):
        gate = jnp.dot(x, w_gate, preferred_element_type=jnp.float32)
        up = jnp.dot(x, w_up, preferred_element_type=jnp.float32)
        hidden = (jax.nn.gelu(gate) * up).astype(jnp.bfloat16)
        term = jnp.dot(hidden, w_down, preferred_element_type=jnp.float32).astype(jnp.bfloat16)
        return lax.psum(term, "tp")

    return jax.shard_map(
        step,
        mesh=mesh,
        in_specs=(P("dp", None), P(None, "tp"), P(None, "tp"), P("tp", None)),
        out_specs=P("dp", None),
        check_vma=False,
    )
```

profile of v0, /device:TPU:21, one launch (start us, length us, event | category | flops | bytes accessed | tf_op | source)
XLA Modules:
  0.0 470.8 jit_solution(9407384691387613924)
XLA Ops:
  6.5 0.0 all-reduce.2.cloned.1.call-start
  6.6 40.6 %fusion.9 = f32[2048,1920]{1,0:T(8,128)} fusion(bf16[2048,3840]{1,0:T(8,128)(2,1)} %param.4, bf16[3840,1920]{1,0:T(8,128)(2,1)} %param.5), kind=kOutput, calls=%fused_computation.11 | convolution fusion | flops 30198988800 | bytes 46202880 | tf_op jit(solution)/shard_map/dot_general | solution.py:9
  47.2 42.2 %fusion.8 = bf16[2048,1920]{1,0:T(8,128)(2,1)S(1)} fusion(f32[2048,1920]{1,0:T(8,128)} %fusion.9, bf16[2048,3840]{1,0:T(8,128)(2,1)} %param.4, bf16[3840,1920]{1,0:T(8,128)(2,1)} %param.6), kind=kOutput, calls=%fused_computation.9 | convolution fusion | flops 30238310400 | bytes 54067200 | tf_op jit(solution)/shard_map/dot_general | solution.py:10
  89.4 37.3 %convolution_convert_fusion = bf16[2048,3840]{1,0:T(8,128)(2,1)} fusion(bf16[2048,1920]{1,0:T(8,128)(2,1)S(1)} %fusion.8, bf16[1920,3840]{1,0:T(8,128)(2,1)} %param.7), kind=kOutput, calls=%fused_computation.10 | convolution fusion | flops 30206853120 | bytes 38338560 | tf_op jit(solution)/shard_map/dot_general | solution.py:12
  126.7 0.1 all-reduce.2.cloned.1.call-update
  126.7 324.0 %all-reduce.2.cloned.1.call-done = bf16[2048,3840]{1,0:T(8,128)(2,1)} async-done(((bf16[2048,3840]{1,0:T(8,128)(2,1)}), bf16[2048,3840]{1,0:T(8,128)(2,1)}) %all-reduce.2.cloned.1.call-update) | async-done | bytes 15728656 | tf_op jit(solution)/shard_map/psum | solution.py:13
  450.7 13.2 %copy.6 = bf16[2048,3840]{1,0:T(8,128)(2,1)} copy(bf16[2048,3840]{1,0:T(8,128)(2,1)} %all-reduce.2.cloned.1.call-done) | data formatting | bytes 31457280
Async XLA Ops:
  6.5 444.2 %all-reduce.2.cloned.1.call-start = ((), (), s32[]{:S(2)}) async-start(), calls=%async_computation | async-start | bytes 31457280 | tf_op jit(solution)/shard_map/psum | solution.py:13
Sparse Core Ops, SparseCore 0:
  126.8 323.8 all-reduce.1
where the time goes:
time: 471 us
  waiting for transfers between devices  324 us (69%)
  matrix products  120 us (25%)
  between operations  13.4 us (3%)
  local copies, waits for them, and re-layouts  13.2 us (3%)
    psum x1, waiting for transfers between devices, step(): return lax.psum(term, 'tp')  324 us
    dot_general x1, matrix products, step(): up = jnp.dot(x, w_up, preferred_element_type=jnp.float32)  42.2 us
    dot_general x1, matrix products, step(): gate = jnp.dot(x, w_gate, preferred_element_type=jnp.float32)  40.6 us
    dot_general x1, matrix products, step(): jnp.dot(hidden, w_down, preferred_element_type=jnp.float32)  37.3 us
    unnamed x1, local copies, waits for them, and re-layouts  13.2 us
  transfers between devices with their start and end apart: 1, of which 1 were waited for; matrix products, arithmetic and copies ran while one was open for 0% of the time, Pallas kernels for 0%

commit v1 on v0

v1 whole, which is shorter than its diff:
```python
import functools

import jax
import jax.numpy as jnp
from jax import lax
from jax.experimental import pallas as pl
from jax.experimental.pallas import tpu as pltpu
from jax.sharding import PartitionSpec as P

CHUNKS = 5
AHEAD = 2
STORES = 8
VMEM_LIMIT = 67_043_328


def gated(gate, up):
    inner = 0.7978845608028654 * (gate + 0.044715 * (gate * gate * gate))
    return gate * (0.5 * (1.0 + jnp.tanh(inner))) * up


def kernel(
    n, x_ref, gate_ref, up_ref, down_ref, y_ref,
    gu_ref, wd_ref, x_buf, hid_ref,
    x_sem, gu_sem, wd_sem, send_sem, recv_sem,
):
    me = lax.axis_index("tp")
    right, left = lax.rem(me + 1, n), lax.rem(me + n - 1, n)
    peers = (right, left)
    block = x_ref.shape[0] // n
    half = block // 2
    tile = gu_ref.shape[2] // 2
    cols = wd_ref.shape[2]

    def rows_of(way, step):
        owner = lax.rem(me + 2 * n - 1 - step, n) if way == 0 else lax.rem(me + 1 + step, n)
        return pl.multiple_of(owner * block + way * half, half)

    def cols_of(k):
        return pl.ds(pl.multiple_of(k * cols, 128), cols)

    def load_x(step):
        return [
            pltpu.make_async_copy(
                x_ref.at[pl.ds(rows_of(way, step), half)],
                x_buf.at[pl.ds(way * half, half)],
                x_sem.at[way],
            )
            for way in (0, 1)
        ]

    def load_gu(j):
        at = pl.ds(pl.multiple_of(j * tile, 128), tile)
        return [
            pltpu.make_async_copy(gate_ref.at[:, at], gu_ref.at[j, :, pl.ds(0, tile)], gu_sem.at[0, j]),
            pltpu.make_async_copy(up_ref.at[:, at], gu_ref.at[j, :, pl.ds(tile, tile)], gu_sem.at[1, j]),
        ]

    def load_wd(k):
        return pltpu.make_async_copy(down_ref.at[:, cols_of(k)], wd_ref.at[k], wd_sem.at[k])

    def remote(way, step, k):
        at = y_ref.at[pl.ds(rows_of(way, step), half), cols_of(k)]
        return pltpu.make_async_remote_copy(
            src_ref=at,
            dst_ref=at,
            send_sem=send_sem.at[way, step, k],
            recv_sem=recv_sem.at[way, step, k],
            device_id={"tp": peers[way]},
            device_id_type=pl.DeviceIdType.MESH,
        )

    def arrive(way, step, k):
        at = y_ref.at[pl.ds(rows_of(way, step + 1), half), cols_of(k)]
        pltpu.make_async_remote_copy(
            src_ref=at,
            dst_ref=at,
            send_sem=send_sem.at[way, step, k],
            recv_sem=recv_sem.at[way, step, k],
            device_id={"tp": peers[way]},
            device_id_type=pl.DeviceIdType.MESH,
        ).wait_recv()

    def hidden(slot, j):
        both = jnp.dot(x_buf[...], gu_ref[j], preferred_element_type=jnp.float32)
        at = pl.ds(pl.multiple_of(j * tile, 128), tile)
        hid_ref[slot, :, at] = gated(both[:, :tile], both[:, tile:]).astype(hid_ref.dtype)

    barrier = pltpu.get_barrier_semaphore()
    for peer in peers:
        pl.semaphore_signal(barrier, inc=1, device_id={"tp": peer}, device_id_type=pl.DeviceIdType.MESH)

    def load(unit):
        @pl.when(unit < CHUNKS)
        def _():
            for copy in load_gu(unit):
                copy.start()

        @pl.when(jnp.logical_and(unit >= CHUNKS, unit < 2 * CHUNKS))
        def _():
            load_wd(unit - CHUNKS).start()

    for copy in load_x(0):
        copy.start()
    for copy in load_gu(0):
        copy.start()
    for copy in load_x(0):
        copy.wait()
    for copy in load_gu(1):
        copy.start()

    @pl.loop(0, CHUNKS)
    def _(j):
        for copy in load_gu(j):
            copy.wait()
        load(j + AHEAD)
        hidden(0, j)

    for copy in load_x(1):
        copy.start()
    pl.semaphore_wait(barrier, 2)

    @pl.loop(0, CHUNKS)
    def _(k):
        load_wd(k).wait()
        load(CHUNKS + AHEAD + k)
        term = jnp.dot(hid_ref[0], wd_ref[k], preferred_element_type=jnp.float32)
        for way in (0, 1):
            at = (pl.ds(rows_of(way, 0), half), cols_of(k))
            y_ref[at] = term[way * half : (way + 1) * half].astype(y_ref.dtype)
            remote(way, 0, k).start()

    for copy in load_x(1):
        copy.wait()

    @pl.loop(0, CHUNKS)
    def _(j):
        hidden(1, j)

    @pl.loop(1, n)
    def _(step):
        slot = lax.rem(step, 2)
        more = step < n - 1

        @pl.when(more)
        def _():
            for copy in load_x(step + 1):
                copy.start()

        @pl.loop(0, CHUNKS)
        def _(k):
            term = jnp.dot(hid_ref[slot], wd_ref[k], preferred_element_type=jnp.float32)
            for way in (0, 1):
                arrive(way, step - 1, k)

            @pl.when(step > 1)
            def _():
                for way in (0, 1):
                    remote(way, step - 2, k).wait_send()

            for way in (0, 1):
                at = (pl.ds(rows_of(way, step), half), cols_of(k))
                total = y_ref[at].astype(jnp.float32) + term[way * half : (way + 1) * half]
                y_ref[at] = total.astype(y_ref.dtype)
                remote(way, step, k).start()

            @pl.when(jnp.logical_and(more, k == 0))
            def _():
                for copy in load_x(step + 1):
                    copy.wait()

            @pl.when(more)
            def _():
                hidden(1 - slot, k)

    @pl.loop(n, 2 * n - 2)
    def _(step):
        @pl.loop(0, CHUNKS)
        def _(k):
            for way in (0, 1):
                arrive(way, step - 1, k)
                remote(way, step - 2, k).wait_send()
                remote(way, step, k).start()

    @pl.loop(0, CHUNKS)
    def _(k):
        for way in (0, 1):
            arrive(way, 2 * n - 3, k)

    @pl.loop(2 * n - 4, 2 * n - 2)
    def _(step):
        @pl.loop(0, CHUNKS)
        def _(k):
            for way in (0, 1):
                remote(way, step, k).wait_send()


def store(y_ref, out_ref, sem):
    rows = y_ref.shape[0] // STORES
    copies = [
        pltpu.make_async_copy(y_ref.at[pl.ds(i * rows, rows)], out_ref.at[pl.ds(i * rows, rows)], sem.at[i])
        for i in range(STORES)
    ]
    for copy in copies:
        copy.start()
    for copy in copies:
        copy.wait()


def solution(mesh):
    n = mesh.shape["tp"]
    hops = 2 * n - 2

    def step(x, w_gate, w_up, w_down):
        rows, width = x.shape
        units = w_gate.shape[1]
        block = rows // n
        y = pl.pallas_call(
            functools.partial(kernel, n),
            out_shape=pltpu.VMEM((rows, width), jnp.bfloat16),
            in_specs=[pl.BlockSpec(memory_space=pl.ANY)] * 4,
            out_specs=pl.BlockSpec(memory_space=pltpu.VMEM),
            scratch_shapes=[
                pltpu.VMEM((CHUNKS, width, 2 * units // CHUNKS), jnp.bfloat16),
                pltpu.VMEM((CHUNKS, units, width // CHUNKS), jnp.bfloat16),
                pltpu.VMEM((block, width), jnp.bfloat16),
                pltpu.VMEM((2, block, units), jnp.bfloat16),
                pltpu.SemaphoreType.DMA((2,)),
                pltpu.SemaphoreType.DMA((2, CHUNKS)),
                pltpu.SemaphoreType.DMA((CHUNKS,)),
                pltpu.SemaphoreType.DMA((2, hops, CHUNKS)),
                pltpu.SemaphoreType.DMA((2, hops, CHUNKS)),
            ],
            compiler_params=pltpu.CompilerParams(
                collective_id=0,
                has_side_effects=True,
                vmem_limit_bytes=VMEM_LIMIT - rows * width * 2,
            ),
        )(x, w_gate, w_up, w_down)
        return pl.pallas_call(
            store,
            out_shape=jax.ShapeDtypeStruct((rows, width), jnp.bfloat16),
            in_specs=[pl.BlockSpec(memory_space=pl.ANY)],
            out_specs=pl.BlockSpec(memory_space=pl.ANY),
            scratch_shapes=[pltpu.SemaphoreType.DMA((STORES,))],
            compiler_params=pltpu.CompilerParams(vmem_limit_bytes=1 << 20),
        )(pltpu.with_memory_space_constraint(y, pltpu.VMEM))

    return jax.shard_map(
        step,
        mesh=mesh,
        in_specs=(P("dp", None), P(None, "tp"), P(None, "tp"), P("tp", None)),
        out_specs=P("dp", None),
        check_vma=False,
    )
```

time: 471 us -> 325 us (0.69)
  Pallas kernels: 0 us -> 325 us
  waiting for transfers between devices: 324 us -> 0 us
  matrix products: 120 us -> 0 us
  between operations: 13.4 us -> 0.01 us
  local copies, waits for them, and re-layouts: 13.2 us -> 0 us
    pallas_call x0 -> x2, Pallas kernels: none -> 325 us  [the longest x1 319 us: step(): pl.pallas_call(functools.partial(kernel, n), out_shape=pltpu.VMEM((rows,...]
    psum x1 -> x0, waiting for transfers between devices: 324 us -> none  [step(): return lax.psum(term, 'tp')]
    dot_general x3 -> x0, matrix products: 120 us -> none  [the longest x1 42.2 us: step(): up = jnp.dot(x, w_up, preferred_element_type=jnp.float32)]
    unnamed x1 -> x0, local copies, waits for them, and re-layouts: 13.2 us -> none
  transfers between devices with their start and end apart: 1 -> 0, of which waited for: 1 -> 0; matrix products, arithmetic and copies ran while one was open for 0% -> 0% of each run, Pallas kernels for 0% -> 0%
where the time goes in v1:
time: 325 us
  Pallas kernels  325 us (100%)
    pallas_call x1, Pallas kernels, step(): pl.pallas_call(functools.partial(kernel, n), out_shape=pltpu.VMEM((rows,...  319 us

profile of v1, /device:TPU:21, one launch (start us, length us, event | category | flops | bytes accessed | tf_op | source)
XLA Modules:
  0.0 324.8 jit_solution(7293634658016688665)
XLA Ops:
  0.0 319.1 %shard_map.46.y_ref = bf16[2048,3840]{1,0:T(8,128)(2,1)S(1)} custom-call(bf16[2048,3840]{1,0:T(8,128)(2,1)} %x_ref.1, bf16[3840,1920]{1,0:T(8,128)(2,1)} %gate_ref.1, bf16[3840,1920]{1,0:T(8,128)(2,1)} %up_ref.1, bf16[1920,3840]{1,0:T(8,128)(2,1)} %down_ref.1), custom_call_target="tpu_custom_call" | custom-call | tf_op jit(solution)/shard_map/pallas_call | solution.py:217
  319.1 5.6 %shard_map.47 = bf16[2048,3840]{1,0:T(8,128)(2,1)} custom-call(bf16[2048,3840]{1,0:T(8,128)(2,1)S(1)} %shard_map.46.y_ref), custom_call_target="tpu_custom_call" | custom-call | tf_op jit(solution)/shard_map/pallas_call | solution.py:239

commit v2 on v1

--- a/solution.py
+++ b/solution.py
@@ -16,6 +16,15 @@
 def gated(gate, up):
     inner = 0.7978845608028654 * (gate + 0.044715 * (gate * gate * gate))
     return gate * (0.5 * (1.0 + jnp.tanh(inner))) * up
+
+
+def rows_of(n, block, me, way, step):
+    owner = lax.rem(me + 2 * n - 1 - step, n) if way == 0 else lax.rem(me + 1 + step, n)
+    return pl.multiple_of(owner * block + way * (block // 2), block // 2)
+
+
+def split(n):
+    return 2 * n - 4 + lax.rem(lax.axis_index("dp"), 2)
 
 
 def kernel(
@@ -31,17 +40,13 @@
     tile = gu_ref.shape[2] // 2
     cols = wd_ref.shape[2]
 
-    def rows_of(way, step):
-        owner = lax.rem(me + 2 * n - 1 - step, n) if way == 0 else lax.rem(me + 1 + step, n)
-        return pl.multiple_of(owner * block + way * half, half)
-
     def cols_of(k):
         return pl.ds(pl.multiple_of(k * cols, 128), cols)
 
     def load_x(step):
         return [
             pltpu.make_async_copy(
-                x_ref.at[pl.ds(rows_of(way, step), half)],
+                x_ref.at[pl.ds(rows_of(n, block, me, way, step), half)],
                 x_buf.at[pl.ds(way * half, half)],
                 x_sem.at[way],
             )
@@ -59,7 +64,7 @@
         return pltpu.make_async_copy(down_ref.at[:, cols_of(k)], wd_ref.at[k], wd_sem.at[k])
 
     def remote(way, step, k):
-        at = y_ref.at[pl.ds(rows_of(way, step), half), cols_of(k)]
+        at = y_ref.at[pl.ds(rows_of(n, block, me, way, step), half), cols_of(k)]
         return pltpu.make_async_remote_copy(
             src_ref=at,
             dst_ref=at,
@@ -70,7 +75,7 @@
         )
 
     def arrive(way, step, k):
-        at = y_ref.at[pl.ds(rows_of(way, step + 1), half), cols_of(k)]
+        at = y_ref.at[pl.ds(rows_of(n, block, me, way, step + 1), half), cols_of(k)]
         pltpu.make_async_remote_copy(
             src_ref=at,
             dst_ref=at,
@@ -125,7 +130,7 @@
         load(CHUNKS + AHEAD + k)
         term = jnp.dot(hid_ref[0], wd_ref[k], preferred_element_type=jnp.float32)
         for way in (0, 1):
-            at = (pl.ds(rows_of(way, 0), half), cols_of(k))
+            at = (pl.ds(rows_of(n, block, me, way, 0), half), cols_of(k))
             y_ref[at] = term[way * half : (way + 1) * half].astype(y_ref.dtype)
             remote(way, 0, k).start()
 
@@ -158,7 +163,7 @@
                     remote(way, step - 2, k).wait_send()
 
             for way in (0, 1):
-                at = (pl.ds(rows_of(way, step), half), cols_of(k))
+                at = (pl.ds(rows_of(n, block, me, way, step), half), cols_of(k))
                 total = y_ref[at].astype(jnp.float32) + term[way * half : (way + 1) * half]
                 y_ref[at] = total.astype(y_ref.dtype)
                 remote(way, step, k).start()
@@ -172,7 +177,9 @@
             def _():
                 hidden(1 - slot, k)
 
-    @pl.loop(n, 2 * n - 2)
+    last = split(n)
+
+    @pl.loop(n, last)
     def _(step):
         @pl.loop(0, CHUNKS)
         def _(k):
@@ -184,14 +191,71 @@
     @pl.loop(0, CHUNKS)
     def _(k):
         for way in (0, 1):
-            arrive(way, 2 * n - 3, k)
-
-    @pl.loop(2 * n - 4, 2 * n - 2)
+            arrive(way, last - 1, k)
+
+    @pl.loop(last - 2, last)
     def _(step):
         @pl.loop(0, CHUNKS)
         def _(k):
             for way in (0, 1):
                 remote(way, step, k).wait_send()
+
+
+def finish(n, y_ref, early_ref, late_ref, send_sem, recv_sem):
+    del early_ref
+    me = lax.axis_index("tp")
+    peers = (lax.rem(me + 1, n), lax.rem(me + n - 1, n))
+    block = y_ref.shape[0] // n
+    half = block // 2
+    cols = y_ref.shape[1] // CHUNKS
+    two = split(n) == 2 * n - 4
+
+    barrier = pltpu.get_barrier_semaphore()
+    for peer in peers:
+        pl.semaphore_signal(barrier, inc=1, device_id={"tp": peer}, device_id_type=pl.DeviceIdType.MESH)
+    pl.semaphore_wait(barrier, 2)
+
+    def remote(way, i, k, stored):
+        at = pl.ds(pl.multiple_of(k * cols, 128), cols)
+        rows = pl.ds(rows_of(n, block, me, way, 2 * n - 4 + i), half)
+        return pltpu.make_async_remote_copy(
+            src_ref=late_ref.at[way, 0, :, at] if stored else y_ref.at[rows, at],
+            dst_ref=late_ref.at[way, i, :, at],
+            send_sem=send_sem.at[way, i, k],
+            recv_sem=recv_sem.at[way, i, k],
+            device_id={"tp": peers[way]},
+            device_id_type=pl.DeviceIdType.MESH,
+        )
+
+    @pl.when(two)
+    def _():
+        @pl.loop(0, CHUNKS)
+        def _(k):
+            for way in (0, 1):
+                remote(way, 0, k, False).start()
+
+        @pl.loop(0, CHUNKS)
+        def _(k):
+            for way in (0, 1):
+                remote(way, 0, k, False).wait_recv()
+                remote(way, 1, k, True).start()
+
+        @pl.loop(0, CHUNKS)
+        def _(k):
+            for way in (0, 1):
+                remote(way, 0, k, False).wait_send()
+
+    @pl.when(jnp.logical_not(two))
+    def _():
+        @pl.loop(0, CHUNKS)
+        def _(k):
+            for way in (0, 1):
+                remote(way, 1, k, False).start()
+
+    @pl.loop(0, CHUNKS)
+    def _(k):
+        for way in (0, 1):
+            remote(way, 1, k, True).wait()
 
 
 def store(y_ref, out_ref, sem):
@@ -204,6 +268,33 @@
         copy.start()
     for copy in copies:
         copy.wait()
+
+
+def store_late(n, early_ref, late_ref, out_ref, sem):
+    del early_ref
+    me = lax.axis_index("tp")
+    block = out_ref.shape[0] // n
+
+    def copy(way, i):
+        rows = pl.ds(rows_of(n, block, me, way, 2 * n - 3 + i), block // 2)
+        return pltpu.make_async_copy(late_ref.at[way, i], out_ref.at[rows], sem.at[way, i])
+
+    two = split(n) == 2 * n - 4
+
+    @pl.when(two)
+    def _():
+        for way in (0, 1):
+            copy(way, 0).start()
+
+    for way in (0, 1):
+        copy(way, 1).start()
+    for way in (0, 1):
+        copy(way, 1).wait()
+
+    @pl.when(two)
+    def _():
+        for way in (0, 1):
+            copy(way, 0).wait()
 
 
 def solution(mesh):
@@ -236,14 +327,39 @@
                 vmem_limit_bytes=VMEM_LIMIT - rows * width * 2,
             ),
         )(x, w_gate, w_up, w_down)
-        return pl.pallas_call(
+        y = pltpu.with_memory_space_constraint(y, pltpu.VMEM)
+        anywhere = pl.BlockSpec(memory_space=pl.ANY)
+        early = pl.pallas_call(
             store,
             out_shape=jax.ShapeDtypeStruct((rows, width), jnp.bfloat16),
-            in_specs=[pl.BlockSpec(memory_space=pl.ANY)],
-            out_specs=pl.BlockSpec(memory_space=pl.ANY),
+            in_specs=[anywhere],
+            out_specs=anywhere,
             scratch_shapes=[pltpu.SemaphoreType.DMA((STORES,))],
             compiler_params=pltpu.CompilerParams(vmem_limit_bytes=1 << 20),
-        )(pltpu.with_memory_space_constraint(y, pltpu.VMEM))
+        )(y)
+        late = pl.pallas_call(
+            functools.partial(finish, n),
+            out_shape=pltpu.VMEM((2, 2, block // 2, width), jnp.bfloat16),
+            in_specs=[anywhere] * 2,
+            out_specs=anywhere,
+            scratch_shapes=[
+                pltpu.SemaphoreType.DMA((2, 2, CHUNKS)),
+                pltpu.SemaphoreType.DMA((2, 2, CHUNKS)),
+            ],
+            compiler_params=pltpu.CompilerParams(
+                collective_id=1, has_side_effects=True, vmem_limit_bytes=1 << 20
+            ),
+        )(y, pltpu.with_memory_space_constraint(early, pltpu.HBM))
+        late = pltpu.with_memory_space_constraint(late, pltpu.VMEM)
+        return pl.pallas_call(
+            functools.partial(store_late, n),
+            out_shape=jax.ShapeDtypeStruct((rows, width), jnp.bfloat16),
+            in_specs=[anywhere] * 2,
+            out_specs=anywhere,
+            input_output_aliases={0: 0},
+            scratch_shapes=[pltpu.SemaphoreType.DMA((2, 2))],
+            compiler_params=pltpu.CompilerParams(vmem_limit_bytes=1 << 20),
+        )(early, late)
 
     return jax.shard_map(
         step,

time: 325 us -> 322 us (level)
  Pallas kernels: 325 us -> 320 us
    pallas_call x1, Pallas kernels: 319 us -> 288 us  [step(): pl.pallas_call(functools.partial(kernel, n), out_shape=pltpu.VMEM((rows,...]
    pallas_call x0 -> x2, Pallas kernels: none -> 26.8 us  [the longest x1 25.4 us: step(): pl.pallas_call(functools.partial(finish, n), out_shape=pltpu.VMEM((2, 2,...]
where the time goes in v2:
time: 322 us; the launch traced here: 320 us
  Pallas kernels  320 us (99%)
    pallas_call x1, Pallas kernels, step(): pl.pallas_call(functools.partial(kernel, n), out_shape=pltpu.VMEM((rows,...  288 us
    pallas_call x1, Pallas kernels, step(): pl.pallas_call(functools.partial(finish, n), out_shape=pltpu.VMEM((2, 2,...  25.4 us

profile of v2, /device:TPU:21, one launch (start us, length us, event | category | flops | bytes accessed | tf_op | source)
XLA Modules:
  0.0 320.4 jit_solution(15955067803300764801)
XLA Ops:
  0.0 288.0 %shard_map.46.y_ref = bf16[2048,3840]{1,0:T(8,128)(2,1)S(1)} custom-call(bf16[2048,3840]{1,0:T(8,128)(2,1)} %x_ref.1, bf16[3840,1920]{1,0:T(8,128)(2,1)} %gate_ref.1, bf16[3840,1920]{1,0:T(8,128)(2,1)} %up_ref.1, bf16[1920,3840]{1,0:T(8,128)(2,1)} %down_ref.1), custom_call_target="tpu_custom_call" | custom-call | tf_op jit(solution)/shard_map/pallas_call | solution.py:308
  288.0 5.6 %shard_map.47.early_ref = bf16[2048,3840]{1,0:T(8,128)(2,1)} custom-call(bf16[2048,3840]{1,0:T(8,128)(2,1)S(1)} %shard_map.46.y_ref), custom_call_target="tpu_custom_call" | custom-call | tf_op jit(solution)/shard_map/pallas_call | solution.py:332
  293.7 25.4 %shard_map.48.late_ref = bf16[2,2,128,3840]{3,2,1,0:T(8,128)(2,1)S(1)} custom-call(bf16[2048,3840]{1,0:T(8,128)(2,1)S(1)} %shard_map.46.y_ref, bf16[2048,3840]{1,0:T(8,128)(2,1)} %shard_map.47.early_ref), custom_call_target="tpu_custom_call" | custom-call | tf_op jit(solution)/shard_map/pallas_call | solution.py:340
  319.1 1.3 shard_map.49
